TPU v7x, 128 devices: a whole 4x4x4 slice. The times are simulated.
128 devices in a mesh: pair: 8 (over x, core), ep: 16 (over z, y).
Axes of the slice: x: 4, y: 4, z: 4, core: 2. Of those that a mesh axis runs over, the one named last changes fastest.
Arguments:
- tokens: bfloat16 [32768, 4096], P(('pair', 'ep')), may hold values from -6 to 6
- expert_of: int32 [32768, 1], P(('pair', 'ep')), may hold values from 0 to 127, as said below
- w_gate: bfloat16 [128, 4096, 768], P(('pair', 'ep')), may hold values from -0.09375 to 0.09375
- w_up: bfloat16 [128, 4096, 768], P(('pair', 'ep')), may hold values from -0.09375 to 0.09375
- w_down: bfloat16 [128, 768, 4096], P(('pair', 'ep')), may hold values from -0.21875 to 0.21875
Outputs:
- mixed: bfloat16 [32768, 4096], P(('pair', 'ep'))
Inputs may be any that keep to these rules, and one draw needn't show every extreme that they name: `expert_of`: the rows of one device (aligned blocks of 256 tokens) name no expert more than 3 times; in every draw one expert, drawn from the seed, is named exactly 3 times in every device's rows.
All inputs are finite; a program needn't handle non-finite values.
Results may differ from a plain program's by a relative error of at most 0.005.
Values may be sent and summed in bfloat16 or wider, within the bound.
No kernel may reach another device: no remote copies, remote signals or barrier semaphores. Data moves between devices by JAX's collectives and lax.ppermute only.
A program may use at most 128 MiB of HBM per device.

v0:
```python
import jax
import jax.numpy as jnp
from jax import lax
from jax.sharding import PartitionSpec as P


def shards(tokens, expert_of, w_gate, w_up, w_down):
    pair_count = lax.axis_size("pair")
    ep_count = lax.axis_size("ep")
    experts = pair_count * ep_count
    tok_rows = tokens.shape[0]
    capacity = tok_rows // experts + tok_rows // (2 * experts)
    routed = expert_of[:, 0]
    onehot = (routed[:, None] == jnp.arange(experts, dtype=jnp.int32)[None, :]).astype(jnp.float32)
    earlier_mask = (jnp.arange(tok_rows)[:, None] > jnp.arange(tok_rows)[None, :]).astype(
        jnp.float32
    )
    before = jnp.dot(earlier_mask, onehot, precision=lax.Precision.HIGHEST)
    slot_index = jnp.sum(before * onehot, axis=1).astype(jnp.int32)
    position = routed * capacity + slot_index
    outgoing = (
        jnp.zeros((experts * capacity, tokens.shape[1]), jnp.bfloat16).at[position].set(tokens)
    )
    parcel = lax.all_to_all(
        outgoing.reshape(experts, capacity, outgoing.shape[1]),
        ("pair", "ep"),
        split_axis=0,
        concat_axis=0,
        tiled=True,
    )
    senders = parcel.shape[0]
    per_sender = parcel.shape[1]
    flat_rows = parcel.reshape(senders * per_sender, parcel.shape[2])
    gate_proj = jnp.dot(flat_rows, w_gate[0], preferred_element_type=jnp.float32)
    up_proj = jnp.dot(flat_rows, w_up[0], preferred_element_type=jnp.float32)
    hidden = (jax.nn.silu(gate_proj) * up_proj).astype(jnp.bfloat16)
    result = jnp.dot(hidden, w_down[0], preferred_element_type=jnp.float32).astype(jnp.bfloat16)
    returned = lax.all_to_all(
        result.reshape(senders, per_sender, result.shape[1]),
        ("pair", "ep"),
        split_axis=0,
        concat_axis=0,
        tiled=True,
    )
    returned = returned.reshape(experts * capacity, returned.shape[2])
    return jnp.take(returned, position, axis=0)


def solution(mesh):
    in_specs = (
        P(("pair", "ep"), None),
        P(("pair", "ep"), None),
        P(("pair", "ep"), None, None),
        P(("pair", "ep"), None, None),
        P(("pair", "ep"), None, None),
    )
    out_specs = P(("pair", "ep"), None)
    return jax.shard_map(shards, mesh=mesh, in_specs=in_specs, out_specs=out_specs, check_vma=False)
```

profile of v0, /device:TPU:1, one launch (start us, length us, event | category | flops | bytes accessed | tf_op | source)
XLA Modules:
  0.0 176.6 jit_solution(17096203641321768983)
XLA Ops:
  0.0 1.0 fusion.17
  1.0 0.7 and_reduce_fusion
  1.7 5.5 %scatter_custom_fusion = bf16[384,4096]{1,0:T(8,128)(2,1)S(1)} fusion(s32[256]{0:T(256)S(1)} %bitcast.22, bf16[256,4096]{1,0:T(8,128)(2,1)} %param.5, bf16[]{:T(256)} %constant.25.clone.1), kind=kCustom, calls=%fused_computation.10 | custom fusion | bytes 3146240 | tf_op jit(solution)/shard_map/scatter | solution.py:22
  7.2 4.4 %reshape.25 = bf16[128,3,4096]{2,1,0:T(4,128)(2,1)} reshape(bf16[384,4096]{1,0:T(8,128)(2,1)S(1)} %scatter_custom_fusion) | data formatting | bytes 6291456 | tf_op jit(solution)/shard_map/reshape | solution.py:25
  11.6 62.7 %all_to_all.10 = bf16[128,3,4096]{2,1,0:T(4,128)(2,1)} all-to-all(bf16[128,3,4096]{2,1,0:T(4,128)(2,1)} %reshape.25), channel_id=1, replica_groups=mesh['pair'=8,'ep'=16] {'pair','ep'}, dimensions={0} | all-to-all | bytes 6291456 | tf_op jit(solution)/shard_map/all_to_all | solution.py:24
  74.3 6.0 %reshape.26 = bf16[384,4096]{1,0:T(8,128)(2,1)S(1)} reshape(bf16[128,3,4096]{2,1,0:T(4,128)(2,1)} %all_to_all.10) | data formatting | bytes 6291456 | tf_op jit(solution)/shard_map/reshape | solution.py:33
  80.3 6.4 %fusion.4 = f32[384,768]{1,0:T(8,128)} fusion(bf16[384,4096]{1,0:T(8,128)(2,1)S(1)} %reshape.26, bf16[1,4096,768]{2,1,0:T(8,128)(2,1)} %param.7), kind=kOutput, calls=%fused_computation.6 | convolution fusion | flops 2415919104 | bytes 10616832 | tf_op jit(solution)/shard_map/dot_general | solution.py:34
  86.7 13.3 %fusion.6 = bf16[384,4096]{1,0:T(8,128)(2,1)} fusion(bf16[1,768,4096]{2,1,0:T(8,128)(2,1)} %param.9, bf16[384,4096]{1,0:T(8,128)(2,1)S(1)} %reshape.26, bf16[1,4096,768]{2,1,0:T(8,128)(2,1)} %param.8, f32[384,768]{1,0:T(8,128)} %fusion.4), kind=kOutput, calls=%fused_computation.8 | convolution fusion | flops 4835180544 | bytes 20054016 | tf_op jit(solution)/shard_map/dot_general | solution.py:37
  100.0 7.1 %reshape.27 = bf16[128,3,4096]{2,1,0:T(4,128)(2,1)} reshape(bf16[384,4096]{1,0:T(8,128)(2,1)} %fusion.6) | data formatting | bytes 6291456 | tf_op jit(solution)/shard_map/reshape | solution.py:39
  107.0 6.4 %all-to-all-start.1 = ((bf16[128,3,4096]{2,1,0:T(4,128)(2,1)}), bf16[128,3,4096]{2,1,0:T(4,128)(2,1)}, u32[]{:S(2)}, u32[]{:S(2)}) async-start(bf16[128,3,4096]{2,1,0:T(4,128)(2,1)} %reshape.27), calls=%async_computation.1 | async-start | bytes 8388608 | tf_op jit(solution)/shard_map/all_to_all | solution.py:38
  113.5 50.8 %all-to-all-done.1 = bf16[128,3,4096]{2,1,0:T(4,128)(2,1)} async-done(((bf16[128,3,4096]{2,1,0:T(4,128)(2,1)}), bf16[128,3,4096]{2,1,0:T(4,128)(2,1)}, u32[]{:S(2)}, u32[]{:S(2)}) %all-to-all-start.1) | async-done | bytes 3145760 | tf_op jit(solution)/shard_map/all_to_all | solution.py:38
  164.3 6.0 %reshape.28 = bf16[384,4096]{1,0:T(8,128)(2,1)S(1)} reshape(bf16[128,3,4096]{2,1,0:T(4,128)(2,1)} %all-to-all-done.1) | data formatting | bytes 6291456 | tf_op jit(solution)/shard_map/reshape | solution.py:45
  170.3 3.2 %gather_fusion = bf16[256,4096]{1,0:T(8,128)(2,1)} fusion(bf16[384,4096]{1,0:T(8,128)(2,1)S(1)} %reshape.28, s32[1024]{0:T(1024)S(1)} %pad_clamp_fusion), kind=kCustom, calls=%fused_computation | custom fusion | bytes 4195328 | tf_op jit(solution)/shard_map/jit(_take)/gather | solution.py:46
  173.4 3.2 %broadcast_select_fusion = bf16[256,4096]{1,0:T(8,128)(2,1)} fusion(bf16[256,4096]{1,0:T(8,128)(2,1)} %gather_fusion, pred[256]{0:T(512)(128)(4,1)S(1)} %get-tuple-element.5), kind=kLoop, calls=%fused_computation.9 | loop fusion | flops 1048576 | bytes 4194560 | tf_op jit(solution)/shard_map/jit(_take)/select_n | solution.py:46
  (2 shorter events, 0.0 us)
Async XLA Ops:
  107.0 57.3 %all-to-all-start.1 = ((bf16[128,3,4096]{2,1,0:T(4,128)(2,1)}), bf16[128,3,4096]{2,1,0:T(4,128)(2,1)}, u32[]{:S(2)}, u32[]{:S(2)}) async-start(bf16[128,3,4096]{2,1,0:T(4,128)(2,1)} %reshape.27), calls=%async_computation.1 | async-start | bytes 8388608 | tf_op jit(solution)/shard_map/all_to_all | solution.py:38
where the time goes:
time: 178 us; the launch traced here: 177 us
  blocking collectives  62.7 us (35%)
  waiting for transfers between devices  50.8 us (29%)
  local copies, waits for them, and re-layouts  32.1 us (18%)
  matrix products  20.7 us (12%)
  starting transfers between devices  6.41 us (4%)
  other arithmetic  3.88 us (2%)
    all_to_all x1, blocking collectives, shards(): lax.all_to_all(outgoing.reshape(experts, capacity, outgoing.shape[1]), ('...  62.7 us
    all_to_all x1, waiting for transfers between devices, shards(): lax.all_to_all(result.reshape(senders, per_sender, result.shape[1]), ('pa...  50.8 us
    dot_general x1, matrix products, shards(): jnp.dot(hidden, w_down[0], preferred_element_type=jnp.float32)  13.3 us
    reshape x1, local copies, waits for them, and re-layouts, shards(): result.reshape(senders, per_sender, result.shape[1])  7.08 us
    all_to_all x1, starting transfers between devices, shards(): lax.all_to_all(result.reshape(senders, per_sender, result.shape[1]), ('pa...  6.41 us
    dot_general x1, matrix products, shards(): jnp.dot(flat_rows, w_gate[0], preferred_element_type=jnp.float32)  6.39 us
    reshape x1, local copies, waits for them, and re-layouts, shards(): flat_rows = parcel.reshape(senders * per_sender, parcel.shape[2])  5.96 us
    reshape x1, local copies, waits for them, and re-layouts, shards(): returned = returned.reshape(experts * capacity, returned.shape[2])  5.96 us
  transfers between devices with their start and end apart: 1, of which 1 were waited for; matrix products, arithmetic and copies ran while one was open for 0% of the time, Pallas kernels for 0%

commit v1 on v0

v1 whole, which is shorter than its diff:
```python
import functools

import jax
import jax.numpy as jnp
from jax import lax
from jax.experimental import pallas as pl
from jax.experimental.pallas import tpu as pltpu
from jax.sharding import PartitionSpec as P

SLOTS = 3
SUB = 8
GROUP = 32
BF16 = jnp.bfloat16
F32 = jnp.float32


def wire_permutation(inverse):
    size = SUB * GROUP
    row = lax.broadcasted_iota(jnp.int32, (size, size), 0)
    col = lax.broadcasted_iota(jnp.int32, (size, size), 1)
    if inverse:
        row, col = col, row
    picked = (row % GROUP) * SUB + row // GROUP
    return (picked == col).astype(F32).astype(BF16)


def dot(a, b):
    return jnp.dot(a, b, preferred_element_type=F32)


def slot_onehots(expert_row, experts):
    tokens = expert_row.shape[1]
    chosen = lax.broadcasted_iota(jnp.int32, (experts, tokens), 0) == expert_row
    earlier = (
        lax.broadcasted_iota(jnp.int32, (tokens, tokens), 0)
        < lax.broadcasted_iota(jnp.int32, (tokens, tokens), 1)
    )
    before = dot(chosen.astype(F32).astype(BF16), earlier.astype(F32).astype(BF16))
    return [
        jnp.where(chosen & (before == float(slot)), 1.0, 0.0).astype(BF16)
        for slot in range(SLOTS)
    ]


def unpack_wire(wire_ref, rows_ref):
    peers = wire_ref.shape[0] // SUB
    width = wire_ref.shape[1] // SLOTS
    size = SUB * GROUP
    perm = wire_permutation(False)
    for b in range(peers // GROUP):
        block = dot(perm, wire_ref[b * size : (b + 1) * size, :]).astype(BF16)
        for slot in range(SLOTS):
            for k in range(SUB):
                rows_ref[
                    slot * peers + b * GROUP : slot * peers + (b + 1) * GROUP,
                    k * width : (k + 1) * width,
                ] = block[k * GROUP : (k + 1) * GROUP, slot * width : (slot + 1) * width]


def stage_rows(part, k, staged_ref):
    peers = part.shape[0] // SLOTS
    width = part.shape[1]
    size = SUB * GROUP
    for b in range(peers // GROUP):
        for slot in range(SLOTS):
            staged_ref[
                b * size + k * GROUP : b * size + (k + 1) * GROUP,
                slot * width : (slot + 1) * width,
            ] = part[slot * peers + b * GROUP : slot * peers + (b + 1) * GROUP]


def pack_wire(staged_ref, wire_ref):
    size = SUB * GROUP
    perm = wire_permutation(True)
    for b in range(staged_ref.shape[0] // size):
        rows = slice(b * size, (b + 1) * size)
        wire_ref[rows, :] = dot(perm, staged_ref[rows, :]).astype(BF16)


def dispatch_kernel(experts, expert_ref, tok_hbm, wire_ref, tok_ref, staged_ref, sems):
    width = tok_ref.shape[1] // SUB
    copies = []
    for k in range(SUB):
        cols = slice(k * width, (k + 1) * width)
        copy = pltpu.make_async_copy(tok_hbm.at[:, cols], tok_ref.at[:, cols], sems.at[k])
        copy.start()
        copies.append(copy)
    onehot = jnp.concatenate(slot_onehots(expert_ref[...], experts), axis=0)
    for k in range(SUB):
        copies[k].wait()
        part = dot(onehot, tok_ref[:, k * width : (k + 1) * width]).astype(BF16)
        stage_rows(part, k, staged_ref)
    pack_wire(staged_ref, wire_ref)


def ffn_kernel(wire_ref, gate_ref, up_ref, down_ref, out_ref, rows_ref, hidden_ref, staged_ref):
    unpack_wire(wire_ref, rows_ref)
    ff = gate_ref.shape[1]
    step = 256

    def hidden_block(i, _):
        cols = pl.ds(pl.multiple_of(i * step, step), step)
        gate = dot(rows_ref[...], gate_ref[:, cols])
        up = dot(rows_ref[...], up_ref[:, cols])
        hidden_ref[:, cols] = (gate / (1.0 + jnp.exp(-gate)) * up).astype(BF16)
        return 0

    lax.fori_loop(0, ff // step, hidden_block, 0)
    width = down_ref.shape[1] // SUB
    for k in range(SUB):
        part = dot(hidden_ref[...], down_ref[:, k * width : (k + 1) * width]).astype(BF16)
        stage_rows(part, k, staged_ref)
    pack_wire(staged_ref, out_ref)


def combine_kernel(experts, expert_ref, wire_ref, out_hbm, rows_ref, out_ref, sems):
    onehot = jnp.concatenate(slot_onehots(expert_ref[...], experts), axis=0)
    pick = onehot.astype(F32).T.astype(BF16)
    unpack_wire(wire_ref, rows_ref)
    width = out_ref.shape[1] // SUB
    copies = []
    for k in range(SUB):
        cols = slice(k * width, (k + 1) * width)
        out_ref[:, cols] = dot(pick, rows_ref[:, cols]).astype(BF16)
        copy = pltpu.make_async_copy(out_ref.at[:, cols], out_hbm.at[:, cols], sems.at[k])
        copy.start()
        copies.append(copy)
    for copy in copies:
        copy.wait()


VMEM = pl.BlockSpec(memory_space=pltpu.VMEM)
ANY = pl.BlockSpec(memory_space=pl.ANY)
HBM = pl.BlockSpec(memory_space=pltpu.HBM)


def shards(tokens, expert_of, w_gate, w_up, w_down):
    axes = ("pair", "ep")
    experts = lax.axis_size("pair") * lax.axis_size("ep")
    tok_rows, d = tokens.shape
    ff = w_gate.shape[2]
    wire_shape = (experts * SUB, SLOTS * d // SUB)
    wire = jax.ShapeDtypeStruct(wire_shape, BF16)
    expert_row = expert_of.reshape(1, tok_rows)

    def exchange(x):
        x = x.reshape(experts, SUB, x.shape[1])
        x = lax.all_to_all(x, axes, split_axis=0, concat_axis=0, tiled=True)
        return x.reshape(wire_shape)

    outgoing = pl.pallas_call(
        functools.partial(dispatch_kernel, experts),
        out_shape=wire,
        in_specs=[VMEM, HBM],
        out_specs=VMEM,
        scratch_shapes=[
            pltpu.VMEM((tok_rows, d), BF16),
            pltpu.VMEM(wire_shape, BF16),
            pltpu.SemaphoreType.DMA((SUB,)),
        ],
        name="dispatch",
    )(expert_row, tokens)
    arrived = exchange(outgoing)
    result = pl.pallas_call(
        ffn_kernel,
        out_shape=wire,
        in_specs=[VMEM] * 4,
        out_specs=VMEM,
        scratch_shapes=[
            pltpu.VMEM((SLOTS * experts, d), BF16),
            pltpu.VMEM((SLOTS * experts, ff), BF16),
            pltpu.VMEM(wire_shape, BF16),
        ],
        compiler_params=pltpu.CompilerParams(vmem_limit_bytes=28 * 2**20),
        name="ffn",
    )(arrived, w_gate[0], w_up[0], w_down[0])
    returned = exchange(result)
    return pl.pallas_call(
        functools.partial(combine_kernel, experts),
        out_shape=jax.ShapeDtypeStruct((tok_rows, d), BF16),
        in_specs=[VMEM, VMEM],
        out_specs=HBM,
        scratch_shapes=[
            pltpu.VMEM((SLOTS * experts, d), BF16),
            pltpu.VMEM((tok_rows, d), BF16),
            pltpu.SemaphoreType.DMA((SUB,)),
        ],
        name="combine",
    )(expert_row, returned)


def solution(mesh):
    spec = P(("pair", "ep"), None)
    weights = P(("pair", "ep"), None, None)
    return jax.shard_map(
        shards,
        mesh=mesh,
        in_specs=(spec, spec, weights, weights, weights),
        out_specs=spec,
        check_vma=False,
    )
```

time: 178 us -> 124 us (0.70)
  waiting for transfers between devices: 50.8 us -> 0 us
  blocking collectives: 62.7 us -> 97.2 us
  local copies, waits for them, and re-layouts: 32.1 us -> 5.58 us
  Pallas kernels: 0 us -> 21.1 us
  matrix products: 20.7 us -> 0 us
  starting transfers between devices: 6.41 us -> 0 us
  other arithmetic: 3.88 us -> 0 us
    all_to_all x1 -> x0, waiting for transfers between devices: 50.8 us -> none  [shards(): lax.all_to_all(result.reshape(senders, per_sender, result.shape[1]), ('pa...]
    all_to_all x1 -> x2, blocking collectives: 62.7 us -> 97.2 us  [exchange(): x = lax.all_to_all(x, axes, split_axis=0, concat_axis=0, tiled=True)]
    reshape x4 -> x0, local copies, waits for them, and re-layouts: 23.5 us -> none  [the longest x1 7.08 us: shards(): result.reshape(senders, per_sender, result.shape[1])]
    pallas_call x0 -> x3, Pallas kernels: none -> 21.1 us  [the longest x1 9.95 us: shards(): pl.pallas_call(ffn_kernel, out_shape=wire, in_specs=[VMEM] * 4, out_specs...]
    dot_general x3 -> x0, matrix products: 20.7 us -> none  [the longest x1 13.3 us: shards(): jnp.dot(hidden, w_down[0], preferred_element_type=jnp.float32)]
    all_to_all x1 -> x0, starting transfers between devices: 6.41 us -> none  [shards(): lax.all_to_all(result.reshape(senders, per_sender, result.shape[1]), ('pa...]
    unnamed x0 -> x6, local copies, waits for them, and re-layouts: none -> 5.58 us
    scatter x1 -> x0, local copies, waits for them, and re-layouts: 5.48 us -> none  [shards(): jnp.zeros((experts * capacity, tokens.shape[1]), jnp.bfloat16).at[position]]
  transfers between devices with their start and end apart: 1 -> 0, of which waited for: 1 -> 0; matrix products, arithmetic and copies ran while one was open for 0% -> 0% of each run, Pallas kernels for 0% -> 0%
where the time goes in v1:
time: 124 us
  blocking collectives  97.2 us (78%)
  Pallas kernels  21.1 us (17%)
  local copies, waits for them, and re-layouts  5.58 us (4%)
    all_to_all x2, blocking collectives, exchange(): x = lax.all_to_all(x, axes, split_axis=0, concat_axis=0, tiled=True)  97.2 us
    pallas_call x1, Pallas kernels, shards(): pl.pallas_call(ffn_kernel, out_shape=wire, in_specs=[VMEM] * 4, out_specs...  9.95 us
    pallas_call x1, Pallas kernels, shards(): pl.pallas_call(functools.partial(dispatch_kernel, experts), out_shape=wir...  6.34 us
    unnamed x6, local copies, waits for them, and re-layouts  5.58 us
    pallas_call x1, Pallas kernels, shards(): pl.pallas_call(functools.partial(combine_kernel, experts), out_shape=jax....  4.78 us

profile of v1, /device:TPU:1, one launch (start us, length us, event | category | flops | bytes accessed | tf_op | source)
XLA Modules:
  0.0 123.8 jit_solution(742180355869511496)
XLA Ops:
  0.0 6.3 %dispatch.1 = bf16[1024,1536]{1,0:T(8,128)(2,1)} custom-call(s32[1,256]{1,0:T(1,128)} %bitcast.15, bf16[256,4096]{1,0:T(8,128)(2,1)} %tok_hbm.1), custom_call_target="tpu_custom_call" | custom-call | tf_op jit(solution)/shard_map/dispatch/pallas_call | solution.py:151
  6.4 0.0 copy-start
  6.4 51.7 %all_to_all.10 = bf16[128,8,1536]{2,1,0:T(8,128)(2,1)S(1)} all-to-all(bf16[128,8,1536]{2,1,0:T(8,128)(2,1)} %bitcast.14), channel_id=1, replica_groups=mesh['pair'=8,'ep'=16] {'pair','ep'}, dimensions={0} | all-to-all | bytes 6291456 | tf_op jit(solution)/shard_map/all_to_all | solution.py:148
  58.1 0.0 copy-done
  58.1 0.0 copy-start.1
  58.1 2.8 %copy-done.1 = bf16[1,4096,768]{2,1,0:T(8,128)(2,1)S(1)} copy-done((bf16[1,4096,768]{2,1,0:T(8,128)(2,1)S(1)}, bf16[1,4096,768]{2,1,0:T(8,128)(2,1)}, u32[]{:S(2)}) %copy-start.1) | copy-done | bytes 6291480
  60.8 0.0 copy-start.2
  60.8 2.8 %copy-done.2 = bf16[1,768,4096]{2,1,0:T(8,128)(2,1)S(1)} copy-done((bf16[1,768,4096]{2,1,0:T(8,128)(2,1)S(1)}, bf16[1,768,4096]{2,1,0:T(8,128)(2,1)}, u32[]{:S(2)}) %copy-start.2) | copy-done | bytes 6291480
  63.6 9.9 %ffn.1 = bf16[1024,1536]{1,0:T(8,128)(2,1)S(1)} custom-call(bf16[1024,1536]{1,0:T(8,128)(2,1)S(1)} %bitcast.8, bf16[4096,768]{1,0:T(8,128)(2,1)S(1)} %bitcast.10, bf16[4096,768]{1,0:T(8,128)(2,1)S(1)} %bitcast.11, bf16[768,4096]{1,0:T(8,128)(2,1)S(1)} %bitcast.12), custom_call_target="tpu_custom_call" | custom-call | tf_op jit(solution)/shard_map/ffn/pallas_call | solution.py:164
  73.6 45.5 %all_to_all.11 = bf16[128,8,1536]{2,1,0:T(8,128)(2,1)} all-to-all(bf16[128,8,1536]{2,1,0:T(8,128)(2,1)S(1)} %bitcast.9), channel_id=1, replica_groups=mesh['pair'=8,'ep'=16] {'pair','ep'}, dimensions={0} | all-to-all | bytes 6291456 | tf_op jit(solution)/shard_map/all_to_all | solution.py:148
  119.1 4.8 %combine.1 = bf16[256,4096]{1,0:T(8,128)(2,1)} custom-call(s32[1,256]{1,0:T(1,128)} %bitcast.16, bf16[1024,1536]{1,0:T(8,128)(2,1)} %bitcast.13), custom_call_target="tpu_custom_call" | custom-call | tf_op jit(solution)/shard_map/combine/pallas_call | solution.py:178
Async XLA Ops:
  6.4 51.7 %copy-start = (bf16[1,4096,768]{2,1,0:T(8,128)(2,1)S(1)}, bf16[1,4096,768]{2,1,0:T(8,128)(2,1)}, u32[]{:S(2)}) copy-start(bf16[1,4096,768]{2,1,0:T(8,128)(2,1)} %param.7) | copy-start | bytes 18874372
  58.1 2.8 %copy-start.1 = (bf16[1,4096,768]{2,1,0:T(8,128)(2,1)S(1)}, bf16[1,4096,768]{2,1,0:T(8,128)(2,1)}, u32[]{:S(2)}) copy-start(bf16[1,4096,768]{2,1,0:T(8,128)(2,1)} %param.8) | copy-start | bytes 18874372
  60.8 2.8 %copy-start.2 = (bf16[1,768,4096]{2,1,0:T(8,128)(2,1)S(1)}, bf16[1,768,4096]{2,1,0:T(8,128)(2,1)}, u32[]{:S(2)}) copy-start(bf16[1,768,4096]{2,1,0:T(8,128)(2,1)} %param.9) | copy-start | bytes 18874372

commit v2 on v1

--- a/solution.py
+++ b/solution.py
@@ -37,7 +37,7 @@
     )
     before = dot(chosen.astype(F32).astype(BF16), earlier.astype(F32).astype(BF16))
     return [
-        jnp.where(chosen & (before == float(slot)), 1.0, 0.0).astype(BF16)
+        jnp.where(chosen & (before == float(slot)), 1.0, 0.0)
         for slot in range(SLOTS)
     ]
 
@@ -77,15 +77,22 @@
         wire_ref[rows, :] = dot(perm, staged_ref[rows, :]).astype(BF16)
 
 
-def dispatch_kernel(experts, expert_ref, tok_hbm, wire_ref, tok_ref, staged_ref, sems):
+def dispatch_kernel(
+    experts, expert_hbm, tok_hbm, wire_ref, pick_ref, expert_ref, tok_ref, staged_ref, sems
+):
     width = tok_ref.shape[1] // SUB
+    expert_copy = pltpu.make_async_copy(expert_hbm, expert_ref, sems.at[SUB])
+    expert_copy.start()
     copies = []
     for k in range(SUB):
         cols = slice(k * width, (k + 1) * width)
         copy = pltpu.make_async_copy(tok_hbm.at[:, cols], tok_ref.at[:, cols], sems.at[k])
         copy.start()
         copies.append(copy)
+    expert_copy.wait()
     onehot = jnp.concatenate(slot_onehots(expert_ref[...], experts), axis=0)
+    pick_ref[...] = onehot.T.astype(BF16)
+    onehot = onehot.astype(BF16)
     for k in range(SUB):
         copies[k].wait()
         part = dot(onehot, tok_ref[:, k * width : (k + 1) * width]).astype(BF16)
@@ -93,19 +100,37 @@
     pack_wire(staged_ref, wire_ref)
 
 
-def ffn_kernel(wire_ref, gate_ref, up_ref, down_ref, out_ref, rows_ref, hidden_ref, staged_ref):
+def ffn_kernel(
+    wire_ref,
+    gate_ref,
+    up_hbm,
+    down_hbm,
+    out_ref,
+    rows_ref,
+    act_ref,
+    hidden_ref,
+    staged_ref,
+    up_ref,
+    down_ref,
+    sems,
+):
+    up_copy = pltpu.make_async_copy(up_hbm, up_ref, sems.at[0])
+    down_copy = pltpu.make_async_copy(down_hbm, down_ref, sems.at[1])
+    up_copy.start()
+    down_copy.start()
     unpack_wire(wire_ref, rows_ref)
     ff = gate_ref.shape[1]
     step = 256
-
-    def hidden_block(i, _):
-        cols = pl.ds(pl.multiple_of(i * step, step), step)
+    for i in range(ff // step):
+        cols = slice(i * step, (i + 1) * step)
         gate = dot(rows_ref[...], gate_ref[:, cols])
+        act_ref[:, cols] = gate / (1.0 + jnp.exp(-gate))
+    up_copy.wait()
+    for i in range(ff // step):
+        cols = slice(i * step, (i + 1) * step)
         up = dot(rows_ref[...], up_ref[:, cols])
-        hidden_ref[:, cols] = (gate / (1.0 + jnp.exp(-gate)) * up).astype(BF16)
-        return 0
-
-    lax.fori_loop(0, ff // step, hidden_block, 0)
+        hidden_ref[:, cols] = (act_ref[:, cols] * up).astype(BF16)
+    down_copy.wait()
     width = down_ref.shape[1] // SUB
     for k in range(SUB):
         part = dot(hidden_ref[...], down_ref[:, k * width : (k + 1) * width]).astype(BF16)
@@ -113,15 +138,13 @@
     pack_wire(staged_ref, out_ref)
 
 
-def combine_kernel(experts, expert_ref, wire_ref, out_hbm, rows_ref, out_ref, sems):
-    onehot = jnp.concatenate(slot_onehots(expert_ref[...], experts), axis=0)
-    pick = onehot.astype(F32).T.astype(BF16)
+def combine_kernel(pick_ref, wire_ref, out_hbm, rows_ref, out_ref, sems):
     unpack_wire(wire_ref, rows_ref)
     width = out_ref.shape[1] // SUB
     copies = []
     for k in range(SUB):
         cols = slice(k * width, (k + 1) * width)
-        out_ref[:, cols] = dot(pick, rows_ref[:, cols]).astype(BF16)
+        out_ref[:, cols] = dot(pick_ref[...], rows_ref[:, cols]).astype(BF16)
         copy = pltpu.make_async_copy(out_ref.at[:, cols], out_hbm.at[:, cols], sems.at[k])
         copy.start()
         copies.append(copy)
@@ -130,8 +153,12 @@
 
 
 VMEM = pl.BlockSpec(memory_space=pltpu.VMEM)
-ANY = pl.BlockSpec(memory_space=pl.ANY)
 HBM = pl.BlockSpec(memory_space=pltpu.HBM)
+SMALL = pltpu.CompilerParams(vmem_limit_bytes=16 * 2**20)
+
+
+def in_hbm(x):
+    return pltpu.with_memory_space_constraint(x, pltpu.HBM)
 
 
 def shards(tokens, expert_of, w_gate, w_up, w_down):
@@ -140,7 +167,7 @@
     tok_rows, d = tokens.shape
     ff = w_gate.shape[2]
     wire_shape = (experts * SUB, SLOTS * d // SUB)
-    wire = jax.ShapeDtypeStruct(wire_shape, BF16)
+    wire = pltpu.VMEM(wire_shape, BF16)
     expert_row = expert_of.reshape(1, tok_rows)
 
     def exchange(x):
@@ -148,35 +175,41 @@
         x = lax.all_to_all(x, axes, split_axis=0, concat_axis=0, tiled=True)
         return x.reshape(wire_shape)
 
-    outgoing = pl.pallas_call(
+    outgoing, pick = pl.pallas_call(
         functools.partial(dispatch_kernel, experts),
-        out_shape=wire,
-        in_specs=[VMEM, HBM],
-        out_specs=VMEM,
+        out_shape=(wire, jax.ShapeDtypeStruct((tok_rows, SLOTS * experts), BF16)),
+        in_specs=[HBM, HBM],
+        out_specs=(VMEM, VMEM),
         scratch_shapes=[
+            pltpu.VMEM((1, tok_rows), jnp.int32),
             pltpu.VMEM((tok_rows, d), BF16),
             pltpu.VMEM(wire_shape, BF16),
-            pltpu.SemaphoreType.DMA((SUB,)),
+            pltpu.SemaphoreType.DMA((SUB + 1,)),
         ],
+        compiler_params=SMALL,
         name="dispatch",
-    )(expert_row, tokens)
+    )(in_hbm(expert_row), in_hbm(tokens))
     arrived = exchange(outgoing)
     result = pl.pallas_call(
         ffn_kernel,
         out_shape=wire,
-        in_specs=[VMEM] * 4,
+        in_specs=[VMEM, VMEM, HBM, HBM],
         out_specs=VMEM,
         scratch_shapes=[
             pltpu.VMEM((SLOTS * experts, d), BF16),
+            pltpu.VMEM((SLOTS * experts, ff), F32),
             pltpu.VMEM((SLOTS * experts, ff), BF16),
             pltpu.VMEM(wire_shape, BF16),
+            pltpu.VMEM((d, ff), BF16),
+            pltpu.VMEM((ff, d), BF16),
+            pltpu.SemaphoreType.DMA((2,)),
         ],
         compiler_params=pltpu.CompilerParams(vmem_limit_bytes=28 * 2**20),
         name="ffn",
-    )(arrived, w_gate[0], w_up[0], w_down[0])
+    )(arrived, w_gate[0], in_hbm(w_up[0]), in_hbm(w_down[0]))
     returned = exchange(result)
     return pl.pallas_call(
-        functools.partial(combine_kernel, experts),
+        combine_kernel,
         out_shape=jax.ShapeDtypeStruct((tok_rows, d), BF16),
         in_specs=[VMEM, VMEM],
         out_specs=HBM,
@@ -185,8 +218,9 @@
             pltpu.VMEM((tok_rows, d), BF16),
             pltpu.SemaphoreType.DMA((SUB,)),
         ],
+        compiler_params=SMALL,
         name="combine",
-    )(expert_row, returned)
+    )(pick, returned)
 
 
 def solution(mesh):

time: 124 us -> 118 us (0.952)
  local copies, waits for them, and re-layouts: 5.58 us -> 0.01 us
    unnamed x6 -> x2, local copies, waits for them, and re-layouts: 5.58 us -> 0.01 us
where the time goes in v2:
time: 118 us; the launch traced here: 117 us
  blocking collectives  96.8 us (82%)
  Pallas kernels  20.5 us (17%)
    all_to_all x2, blocking collectives, exchange(): x = lax.all_to_all(x, axes, split_axis=0, concat_axis=0, tiled=True)  96.8 us
    pallas_call x1, Pallas kernels, shards(): pl.pallas_call(ffn_kernel, out_shape=wire, in_specs=[VMEM, VMEM, HBM, HBM...  13.6 us
    pallas_call x1, Pallas kernels, shards(): pl.pallas_call(functools.partial(dispatch_kernel, experts), out_shape=(wi...  4.06 us
    pallas_call x1, Pallas kernels, shards(): pl.pallas_call(combine_kernel, out_shape=jax.ShapeDtypeStruct((tok_rows,...  2.85 us

profile of v2, /device:TPU:1, one launch (start us, length us, event | category | flops | bytes accessed | tf_op | source)
XLA Modules:
  0.0 117.4 jit_solution(2571417375340950314)
XLA Ops:
  0.0 4.1 %dispatch.1 = (bf16[1024,1536]{1,0:T(8,128)(2,1)S(1)}, bf16[256,384]{1,0:T(8,128)(2,1)S(1)}) custom-call(s32[1,256]{1,0:T(1,128)} %bitcast.15, bf16[256,4096]{1,0:T(8,128)(2,1)} %tok_hbm.1), custom_call_target="tpu_custom_call" | custom-call | tf_op jit(solution)/shard_map/dispatch/pallas_call | solution.py:178
  4.1 0.0 copy-start
  4.1 51.5 %all_to_all.10 = bf16[128,8,1536]{2,1,0:T(8,128)(2,1)S(1)} all-to-all(bf16[128,8,1536]{2,1,0:T(8,128)(2,1)S(1)} %bitcast.12), channel_id=1, replica_groups=mesh['pair'=8,'ep'=16] {'pair','ep'}, dimensions={0} | all-to-all | bytes 6291456 | tf_op jit(solution)/shard_map/all_to_all | solution.py:175
  55.6 0.0 copy-done
  55.6 13.6 %ffn.1 = bf16[1024,1536]{1,0:T(8,128)(2,1)S(1)} custom-call(bf16[1024,1536]{1,0:T(8,128)(2,1)S(1)} %bitcast.8, bf16[4096,768]{1,0:T(8,128)(2,1)S(1)} %bitcast.11, bf16[4096,768]{1,0:T(8,128)(2,1)} %bitcast.13, bf16[768,4096]{1,0:T(8,128)(2,1)} %bitcast.14), custom_call_target="tpu_custom_call" | custom-call | tf_op jit(solution)/shard_map/ffn/pallas_call | solution.py:193
  69.2 45.4 %all_to_all.11 = bf16[128,8,1536]{2,1,0:T(8,128)(2,1)S(1)} all-to-all(bf16[128,8,1536]{2,1,0:T(8,128)(2,1)S(1)} %bitcast.9), channel_id=1, replica_groups=mesh['pair'=8,'ep'=16] {'pair','ep'}, dimensions={0} | all-to-all | bytes 6291456 | tf_op jit(solution)/shard_map/all_to_all | solution.py:175
  114.6 2.9 %combine.1 = bf16[256,4096]{1,0:T(8,128)(2,1)} custom-call(bf16[256,384]{1,0:T(8,128)(2,1)S(1)} %get-tuple-element.7.pick_ref, bf16[1024,1536]{1,0:T(8,128)(2,1)S(1)} %bitcast.10), custom_call_target="tpu_custom_call" | custom-call | tf_op jit(solution)/shard_map/combine/pallas_call | solution.py:211
Async XLA Ops:
  4.1 51.5 %copy-start = (bf16[1,4096,768]{2,1,0:T(8,128)(2,1)S(1)}, bf16[1,4096,768]{2,1,0:T(8,128)(2,1)}, u32[]{:S(2)}) copy-start(bf16[1,4096,768]{2,1,0:T(8,128)(2,1)} %param.7) | copy-start | bytes 18874372

commit v3 on v2

--- a/solution.py
+++ b/solution.py
@@ -103,21 +103,14 @@
 def ffn_kernel(
     wire_ref,
     gate_ref,
-    up_hbm,
-    down_hbm,
+    up_ref,
+    down_ref,
     out_ref,
     rows_ref,
     act_ref,
     hidden_ref,
     staged_ref,
-    up_ref,
-    down_ref,
-    sems,
 ):
-    up_copy = pltpu.make_async_copy(up_hbm, up_ref, sems.at[0])
-    down_copy = pltpu.make_async_copy(down_hbm, down_ref, sems.at[1])
-    up_copy.start()
-    down_copy.start()
     unpack_wire(wire_ref, rows_ref)
     ff = gate_ref.shape[1]
     step = 256
@@ -125,12 +118,10 @@
         cols = slice(i * step, (i + 1) * step)
         gate = dot(rows_ref[...], gate_ref[:, cols])
         act_ref[:, cols] = gate / (1.0 + jnp.exp(-gate))
-    up_copy.wait()
     for i in range(ff // step):
         cols = slice(i * step, (i + 1) * step)
         up = dot(rows_ref[...], up_ref[:, cols])
         hidden_ref[:, cols] = (act_ref[:, cols] * up).astype(BF16)
-    down_copy.wait()
     width = down_ref.shape[1] // SUB
     for k in range(SUB):
         part = dot(hidden_ref[...], down_ref[:, k * width : (k + 1) * width]).astype(BF16)
@@ -187,26 +178,24 @@
             pltpu.SemaphoreType.DMA((SUB + 1,)),
         ],
         compiler_params=SMALL,
+        cost_estimate=pl.CostEstimate(flops=40 * 10**9, bytes_accessed=10**6, transcendentals=0),
         name="dispatch",
     )(in_hbm(expert_row), in_hbm(tokens))
     arrived = exchange(outgoing)
     result = pl.pallas_call(
         ffn_kernel,
         out_shape=wire,
-        in_specs=[VMEM, VMEM, HBM, HBM],
+        in_specs=[VMEM, VMEM, VMEM, VMEM],
         out_specs=VMEM,
         scratch_shapes=[
             pltpu.VMEM((SLOTS * experts, d), BF16),
             pltpu.VMEM((SLOTS * experts, ff), F32),
             pltpu.VMEM((SLOTS * experts, ff), BF16),
             pltpu.VMEM(wire_shape, BF16),
-            pltpu.VMEM((d, ff), BF16),
-            pltpu.VMEM((ff, d), BF16),
-            pltpu.SemaphoreType.DMA((2,)),
         ],
         compiler_params=pltpu.CompilerParams(vmem_limit_bytes=28 * 2**20),
         name="ffn",
-    )(arrived, w_gate[0], in_hbm(w_up[0]), in_hbm(w_down[0]))
+    )(arrived, w_gate[0], w_up[0], w_down[0])
     returned = exchange(result)
     return pl.pallas_call(
         combine_kernel,

time: 118 us -> 113 us (0.958)
  Pallas kernels: 20.5 us -> 16.2 us
    pallas_call x1, Pallas kernels: 13.6 us -> 9.16 us  [shards(): pl.pallas_call(ffn_kernel, out_shape=wire, in_specs=[VMEM, VMEM, VMEM, VM...]
where the time goes in v3:
time: 113 us
  blocking collectives  96.9 us (86%)
  Pallas kernels  16.2 us (14%)
    all_to_all x2, blocking collectives, exchange(): x = lax.all_to_all(x, axes, split_axis=0, concat_axis=0, tiled=True)  96.9 us
    pallas_call x1, Pallas kernels, shards(): pl.pallas_call(ffn_kernel, out_shape=wire, in_specs=[VMEM, VMEM, VMEM, VM...  9.16 us
    pallas_call x1, Pallas kernels, shards(): pl.pallas_call(functools.partial(dispatch_kernel, experts), out_shape=(wi...  4.19 us
    pallas_call x1, Pallas kernels, shards(): pl.pallas_call(combine_kernel, out_shape=jax.ShapeDtypeStruct((tok_rows,...  2.85 us

profile of v3, /device:TPU:1, one launch (start us, length us, event | category | flops | bytes accessed | tf_op | source)
XLA Modules:
  0.0 113.2 jit_solution(4377052463232292822)
XLA Ops:
  0.0 0.0 slice-start
  0.0 0.0 slice-start.2
  0.0 0.0 slice-start.4
  0.0 0.0 slice-start.1
  0.0 0.0 slice-start.3
  0.0 0.0 slice-start.5
  0.0 4.2 %dispatch.1 = (bf16[1024,1536]{1,0:T(8,128)(2,1)S(1)}, bf16[256,384]{1,0:T(8,128)(2,1)S(1)}) custom-call(s32[1,256]{1,0:T(1,128)} %bitcast.21, bf16[256,4096]{1,0:T(8,128)(2,1)} %tok_hbm.1), custom_call_target="tpu_custom_call" | custom-call | flops 40000000000 | bytes 1000000 | tf_op jit(solution)/shard_map/dispatch/pallas_call | solution.py:169
  4.2 51.5 %all_to_all.10 = bf16[128,8,1536]{2,1,0:T(8,128)(2,1)S(1)} all-to-all(bf16[128,8,1536]{2,1,0:T(8,128)(2,1)S(1)} %bitcast.20), channel_id=1, replica_groups=mesh['pair'=8,'ep'=16] {'pair','ep'}, dimensions={0} | all-to-all | bytes 6291456 | tf_op jit(solution)/shard_map/all_to_all | solution.py:166
  55.8 0.0 slice-done
  55.8 0.0 slice-done.2
  55.8 0.0 slice-done.4
  55.8 0.0 slice-done.1
  55.8 0.0 slice-done.3
  55.8 0.0 slice-done.5
  55.8 9.2 %ffn.1 = bf16[1024,1536]{1,0:T(8,128)(2,1)S(1)} custom-call(bf16[1024,1536]{1,0:T(8,128)(2,1)S(1)} %bitcast.8, bf16[4096,768]{1,0:T(8,128)(2,1)S(1)} %bitcast.13, bf16[4096,768]{1,0:T(8,128)(2,1)S(1)} %bitcast.16, bf16[768,4096]{1,0:T(8,128)(2,1)S(1)} %bitcast.19), custom_call_target="tpu_custom_call" | custom-call | tf_op jit(solution)/shard_map/ffn/pallas_call | solution.py:185
  65.0 45.4 %all_to_all.11 = bf16[128,8,1536]{2,1,0:T(8,128)(2,1)S(1)} all-to-all(bf16[128,8,1536]{2,1,0:T(8,128)(2,1)S(1)} %bitcast.9), channel_id=1, replica_groups=mesh['pair'=8,'ep'=16] {'pair','ep'}, dimensions={0} | all-to-all | bytes 6291456 | tf_op jit(solution)/shard_map/all_to_all | solution.py:166
  110.3 2.9 %combine.1 = bf16[256,4096]{1,0:T(8,128)(2,1)} custom-call(bf16[256,384]{1,0:T(8,128)(2,1)S(1)} %get-tuple-element.7.pick_ref, bf16[1024,1536]{1,0:T(8,128)(2,1)S(1)} %bitcast.10), custom_call_target="tpu_custom_call" | custom-call | tf_op jit(solution)/shard_map/combine/pallas_call | solution.py:200
  (3 shorter events, 0.0 us)
Async XLA Ops:
  0.0 55.8 %slice-start = ((s8[6291456]{0:T(1024)(128)(4,1)}), s8[4194304]{0:T(1024)(128)(4,1)S(1)}, s32[]{:S(2)}) async-start(s8[6291456]{0:T(1024)(128)(4,1)} %bitcast.11), calls=%async_computation.2 | async-start | bytes 8388608
  0.0 55.8 %slice-start.2 = ((s8[6291456]{0:T(1024)(128)(4,1)}), s8[4194304]{0:T(1024)(128)(4,1)S(1)}, s32[]{:S(2)}) async-start(s8[6291456]{0:T(1024)(128)(4,1)} %bitcast.14), calls=%async_computation.4 | async-start | bytes 8388608
  0.0 55.8 %slice-start.4 = ((s8[6291456]{0:T(1024)(128)(4,1)}), s8[4194304]{0:T(1024)(128)(4,1)S(1)}, s32[]{:S(2)}) async-start(s8[6291456]{0:T(1024)(128)(4,1)} %bitcast.17), calls=%async_computation.6 | async-start | bytes 8388608
  0.0 55.8 %slice-start.1 = ((s8[6291456]{0:T(1024)(128)(4,1)}), s8[2097152]{0:T(1024)(128)(4,1)S(1)}, s32[]{:S(2)}) async-start(s8[6291456]{0:T(1024)(128)(4,1)} %bitcast.11), calls=%async_computation.3 | async-start | bytes 4194304
  0.0 55.8 %slice-start.3 = ((s8[6291456]{0:T(1024)(128)(4,1)}), s8[2097152]{0:T(1024)(128)(4,1)S(1)}, s32[]{:S(2)}) async-start(s8[6291456]{0:T(1024)(128)(4,1)} %bitcast.14), calls=%async_computation.5 | async-start | bytes 4194304
  0.0 55.8 %slice-start.5 = ((s8[6291456]{0:T(1024)(128)(4,1)}), s8[2097152]{0:T(1024)(128)(4,1)S(1)}, s32[]{:S(2)}) async-start(s8[6291456]{0:T(1024)(128)(4,1)} %bitcast.17), calls=%async_computation.7 | async-start | bytes 4194304

commit v4 on v3

--- a/solution.py
+++ b/solution.py
@@ -9,6 +9,7 @@
 
 SLOTS = 3
 SUB = 8
+LANES = 128
 GROUP = 32
 BF16 = jnp.bfloat16
 F32 = jnp.float32
@@ -69,6 +70,25 @@
             ] = part[slot * peers + b * GROUP : slot * peers + (b + 1) * GROUP]
 
 
+def spread_rows(part, k, spread_ref):
+    peers = part.shape[0] // SLOTS
+    tiles = part.shape[1] // LANES
+    for slot in range(SLOTS):
+        for tile in range(tiles):
+            spread_ref[slot * tiles + tile, pl.ds(k, peers, stride=SUB), :] = part[
+                slot * peers : (slot + 1) * peers, tile * LANES : (tile + 1) * LANES
+            ]
+
+
+def narrow_rows(spread_ref, wire_ref, first, width):
+    full = wire_ref.shape[1] // SLOTS
+    tiles = width // LANES
+    for slot in range(SLOTS):
+        for tile in range(tiles):
+            start = slot * full + first + tile * LANES
+            wire_ref[:, start : start + LANES] = spread_ref[slot * tiles + tile].astype(BF16)
+
+
 def pack_wire(staged_ref, wire_ref):
     size = SUB * GROUP
     perm = wire_permutation(True)
@@ -84,20 +104,24 @@
     expert_copy = pltpu.make_async_copy(expert_hbm, expert_ref, sems.at[SUB])
     expert_copy.start()
     copies = []
+    part = tok_ref.shape[0] // SUB
     for k in range(SUB):
-        cols = slice(k * width, (k + 1) * width)
-        copy = pltpu.make_async_copy(tok_hbm.at[:, cols], tok_ref.at[:, cols], sems.at[k])
+        rows = slice(k * part, (k + 1) * part)
+        copy = pltpu.make_async_copy(tok_hbm.at[rows], tok_ref.at[rows], sems.at[k])
         copy.start()
         copies.append(copy)
     expert_copy.wait()
     onehot = jnp.concatenate(slot_onehots(expert_ref[...], experts), axis=0)
     pick_ref[...] = onehot.T.astype(BF16)
     onehot = onehot.astype(BF16)
-    for k in range(SUB):
-        copies[k].wait()
-        part = dot(onehot, tok_ref[:, k * width : (k + 1) * width]).astype(BF16)
-        stage_rows(part, k, staged_ref)
-    pack_wire(staged_ref, wire_ref)
+    for copy in copies:
+        copy.wait()
+    half = width // 2
+    for h in range(2):
+        for k in range(SUB):
+            first = k * width + h * half
+            spread_rows(dot(onehot, tok_ref[:, first : first + half]), k, staged_ref.at[h])
+        narrow_rows(staged_ref.at[h], wire_ref, h * half, half)
 
 
 def ffn_kernel(
@@ -107,7 +131,6 @@
     down_ref,
     out_ref,
     rows_ref,
-    act_ref,
     hidden_ref,
     staged_ref,
 ):
@@ -117,16 +140,16 @@
     for i in range(ff // step):
         cols = slice(i * step, (i + 1) * step)
         gate = dot(rows_ref[...], gate_ref[:, cols])
-        act_ref[:, cols] = gate / (1.0 + jnp.exp(-gate))
-    for i in range(ff // step):
-        cols = slice(i * step, (i + 1) * step)
         up = dot(rows_ref[...], up_ref[:, cols])
-        hidden_ref[:, cols] = (act_ref[:, cols] * up).astype(BF16)
+        hidden_ref[:, cols] = (gate / (1.0 + jnp.exp(-gate)) * up).astype(BF16)
     width = down_ref.shape[1] // SUB
-    for k in range(SUB):
-        part = dot(hidden_ref[...], down_ref[:, k * width : (k + 1) * width]).astype(BF16)
-        stage_rows(part, k, staged_ref)
-    pack_wire(staged_ref, out_ref)
+    half = width // 2
+    for h in range(2):
+        for k in range(SUB):
+            first = k * width + h * half
+            part = dot(hidden_ref[...], down_ref[:, first : first + half])
+            spread_rows(part, k, staged_ref.at[h])
+        narrow_rows(staged_ref.at[h], out_ref, h * half, half)
 
 
 def combine_kernel(pick_ref, wire_ref, out_hbm, rows_ref, out_ref, sems):
@@ -145,7 +168,7 @@
 
 VMEM = pl.BlockSpec(memory_space=pltpu.VMEM)
 HBM = pl.BlockSpec(memory_space=pltpu.HBM)
-SMALL = pltpu.CompilerParams(vmem_limit_bytes=16 * 2**20)
+SMALL = pltpu.CompilerParams(vmem_limit_bytes=20 * 2**20)
 
 
 def in_hbm(x):
@@ -174,7 +197,7 @@
         scratch_shapes=[
             pltpu.VMEM((1, tok_rows), jnp.int32),
             pltpu.VMEM((tok_rows, d), BF16),
-            pltpu.VMEM(wire_shape, BF16),
+            pltpu.VMEM((2, d // SUB // 2 // LANES * SLOTS, experts * SUB, LANES), F32),
             pltpu.SemaphoreType.DMA((SUB + 1,)),
         ],
         compiler_params=SMALL,
@@ -189,9 +212,8 @@
         out_specs=VMEM,
         scratch_shapes=[
             pltpu.VMEM((SLOTS * experts, d), BF16),
-            pltpu.VMEM((SLOTS * experts, ff), F32),
             pltpu.VMEM((SLOTS * experts, ff), BF16),
-            pltpu.VMEM(wire_shape, BF16),
+            pltpu.VMEM((2, d // SUB // 2 // LANES * SLOTS, experts * SUB, LANES), F32),
         ],
         compiler_params=pltpu.CompilerParams(vmem_limit_bytes=28 * 2**20),
         name="ffn",

time: 113 us -> 112 us (level)
  no operation moved by 1% of the time
where the time goes in v4:
time: 112 us
  blocking collectives  96.9 us (87%)
  Pallas kernels  15.3 us (14%)
    all_to_all x2, blocking collectives, exchange(): x = lax.all_to_all(x, axes, split_axis=0, concat_axis=0, tiled=True)  96.9 us
    pallas_call x1, Pallas kernels, shards(): pl.pallas_call(ffn_kernel, out_shape=wire, in_specs=[VMEM, VMEM, VMEM, VM...  8.99 us
    pallas_call x1, Pallas kernels, shards(): pl.pallas_call(functools.partial(dispatch_kernel, experts), out_shape=(wi...  3.48 us
    pallas_call x1, Pallas kernels, shards(): pl.pallas_call(combine_kernel, out_shape=jax.ShapeDtypeStruct((tok_rows,...  2.85 us

profile of v4, /device:TPU:1, one launch (start us, length us, event | category | flops | bytes accessed | tf_op | source)
XLA Modules:
  0.0 112.3 jit_solution(2777035689922412433)
XLA Ops:
  0.0 0.0 slice-start
  0.0 0.0 slice-start.2
  0.0 0.0 slice-start.4
  0.0 0.0 slice-start.1
  0.0 0.0 slice-start.3
  0.0 0.0 slice-start.5
  0.0 3.5 %dispatch.1 = (bf16[1024,1536]{1,0:T(8,128)(2,1)S(1)}, bf16[256,384]{1,0:T(8,128)(2,1)S(1)}) custom-call(s32[1,256]{1,0:T(1,128)} %bitcast.21, bf16[256,4096]{1,0:T(8,128)(2,1)} %tok_hbm.1), custom_call_target="tpu_custom_call" | custom-call | flops 40000000000 | bytes 1000000 | tf_op jit(solution)/shard_map/dispatch/pallas_call | solution.py:192
  3.5 51.5 %all_to_all.10 = bf16[128,8,1536]{2,1,0:T(8,128)(2,1)S(1)} all-to-all(bf16[128,8,1536]{2,1,0:T(8,128)(2,1)S(1)} %bitcast.20), channel_id=1, replica_groups=mesh['pair'=8,'ep'=16] {'pair','ep'}, dimensions={0} | all-to-all | bytes 6291456 | tf_op jit(solution)/shard_map/all_to_all | solution.py:189
  55.0 0.0 slice-done
  55.0 0.0 slice-done.2
  55.0 0.0 slice-done.4
  55.0 0.0 slice-done.1
  55.0 0.0 slice-done.3
  55.0 0.0 slice-done.5
  55.1 9.0 %ffn.1 = bf16[1024,1536]{1,0:T(8,128)(2,1)S(1)} custom-call(bf16[1024,1536]{1,0:T(8,128)(2,1)S(1)} %bitcast.8, bf16[4096,768]{1,0:T(8,128)(2,1)S(1)} %bitcast.13, bf16[4096,768]{1,0:T(8,128)(2,1)S(1)} %bitcast.16, bf16[768,4096]{1,0:T(8,128)(2,1)S(1)} %bitcast.19), custom_call_target="tpu_custom_call" | custom-call | tf_op jit(solution)/shard_map/ffn/pallas_call | solution.py:208
  64.1 45.4 %all_to_all.11 = bf16[128,8,1536]{2,1,0:T(8,128)(2,1)S(1)} all-to-all(bf16[128,8,1536]{2,1,0:T(8,128)(2,1)S(1)} %bitcast.9), channel_id=1, replica_groups=mesh['pair'=8,'ep'=16] {'pair','ep'}, dimensions={0} | all-to-all | bytes 6291456 | tf_op jit(solution)/shard_map/all_to_all | solution.py:189
  109.4 2.9 %combine.1 = bf16[256,4096]{1,0:T(8,128)(2,1)} custom-call(bf16[256,384]{1,0:T(8,128)(2,1)S(1)} %get-tuple-element.7.pick_ref, bf16[1024,1536]{1,0:T(8,128)(2,1)S(1)} %bitcast.10), custom_call_target="tpu_custom_call" | custom-call | tf_op jit(solution)/shard_map/combine/pallas_call | solution.py:222
  (3 shorter events, 0.0 us)
Async XLA Ops:
  0.0 55.0 %slice-start = ((s8[6291456]{0:T(1024)(128)(4,1)}), s8[4194304]{0:T(1024)(128)(4,1)S(1)}, s32[]{:S(2)}) async-start(s8[6291456]{0:T(1024)(128)(4,1)} %bitcast.11), calls=%async_computation.2 | async-start | bytes 8388608
  0.0 55.0 %slice-start.2 = ((s8[6291456]{0:T(1024)(128)(4,1)}), s8[4194304]{0:T(1024)(128)(4,1)S(1)}, s32[]{:S(2)}) async-start(s8[6291456]{0:T(1024)(128)(4,1)} %bitcast.14), calls=%async_computation.4 | async-start | bytes 8388608
  0.0 55.0 %slice-start.4 = ((s8[6291456]{0:T(1024)(128)(4,1)}), s8[4194304]{0:T(1024)(128)(4,1)S(1)}, s32[]{:S(2)}) async-start(s8[6291456]{0:T(1024)(128)(4,1)} %bitcast.17), calls=%async_computation.6 | async-start | bytes 8388608
  0.0 55.0 %slice-start.1 = ((s8[6291456]{0:T(1024)(128)(4,1)}), s8[2097152]{0:T(1024)(128)(4,1)S(1)}, s32[]{:S(2)}) async-start(s8[6291456]{0:T(1024)(128)(4,1)} %bitcast.11), calls=%async_computation.3 | async-start | bytes 4194304
  0.0 55.0 %slice-start.3 = ((s8[6291456]{0:T(1024)(128)(4,1)}), s8[2097152]{0:T(1024)(128)(4,1)S(1)}, s32[]{:S(2)}) async-start(s8[6291456]{0:T(1024)(128)(4,1)} %bitcast.14), calls=%async_computation.5 | async-start | bytes 4194304
  0.0 55.0 %slice-start.5 = ((s8[6291456]{0:T(1024)(128)(4,1)}), s8[2097152]{0:T(1024)(128)(4,1)S(1)}, s32[]{:S(2)}) async-start(s8[6291456]{0:T(1024)(128)(4,1)} %bitcast.17), calls=%async_computation.7 | async-start | bytes 4194304
